TPU v7x, 256 devices: a 2x2x32 block of a 4x8x32 slice. The times are simulated.
256 devices in a mesh: img: 4 (over y, x), rows: 64 (over z, core).
Axes of the slice: x: 2, y: 2, z: 32, core: 2. Of those that a mesh axis runs over, the one named last changes fastest.
The devices are a block of a 4x8x32 slice.
Arguments:
- hidden_states: bfloat16 [3, 32768, 1024], P(None, ('img', 'rows')), parts along dimension 1, may hold values from -6 to 6
- cell_of: int32 [8192], replicated, may hold values from 0 to 8191, as said below
- proj_four_weight: bfloat16 [1024, 256], replicated, may hold values from -0.1875 to 0.1875
- proj_four_bias: float32 [256], replicated, may hold values from -3 to 3
- proj_two_weight: bfloat16 [1024, 512], replicated, may hold values from -0.1875 to 0.1875
- proj_two_bias: float32 [512], replicated, may hold values from -3 to 3
- proj_same_weight: bfloat16 [1024, 1024], replicated, may hold values from -0.1875 to 0.1875
- proj_same_bias: float32 [1024], replicated, may hold values from -3 to 3
- up4_weight: bfloat16 [256, 4096], replicated, may hold values from -0.375 to 0.375
- up4_bias: float32 [256], replicated, may hold values from -3 to 3
- up2_weight: bfloat16 [512, 2048], replicated, may hold values from -0.25 to 0.25
- up2_bias: float32 [512], replicated, may hold values from -3 to 3
- join_weight: bfloat16 [3, 3, 256, 256], replicated, may hold values from -0.125 to 0.125
Outputs:
- joined_four: bfloat16 [2048, 256, 256], P(('img', 'rows')), parts along dimension 0
- upsampled_two: bfloat16 [1024, 128, 512], P(('img', 'rows')), parts along dimension 0
- same_scale: bfloat16 [512, 64, 1024], P(('img', 'rows')), parts along dimension 0
There are 4 independent parts, one for each index of `img`. A program takes and returns all parts, laid end to end along the dimension named above; an argument that names none is the same for every part. Nothing has to cross between parts.
Inputs may be any that keep to these rules, and one draw needn't show every extreme that they name: `cell_of`: a permutation of the cells 0 to 8191; the sequence positions k * 128 to (k + 1) * 128 - 1 hold exactly 2 cells of every block of 128 consecutive cells.
All inputs are finite; a program needn't handle non-finite values.
Results may differ from a plain program's by a relative error of at most 0.0057.
Values may be sent and summed in bfloat16 or wider, within the bound.
A program may use at most 64 MiB of HBM per device.

v0:
```python
import jax
import jax.numpy as jnp
from jax import lax
from jax.sharding import PartitionSpec as P

GRID_W = 64


def side_by_side(arrays, axis, split_dim, concat_dim, along):
    both = jnp.concatenate(arrays, axis=along)
    whole, at, finished = (
        lax.all_to_all(both, axis, split_axis=split_dim, concat_axis=concat_dim, tiled=True),
        0,
        [],
    )
    for a in arrays:
        finished.append(lax.slice_in_dim(whole, at, at + a.shape[along], axis=along))
        at += a.shape[along]
    return tuple(finished)


def with_halo(cells, sides, width):
    for axis, dim in sides:
        count = lax.axis_size(axis)
        ends = count - 1
        head = lax.slice_in_dim(cells, 0, width, axis=dim)
        tail = lax.slice_in_dim(cells, cells.shape[dim] - width, cells.shape[dim], axis=dim)
        cells = jnp.concatenate(
            [
                lax.ppermute(tail, axis, [(i, (i + 1) % count) for i in range(ends)]),
                cells,
                lax.ppermute(head, axis, [((i + 1) % count, i) for i in range(ends)]),
            ],
            axis=dim,
        )
    return cells


def expand(proj, weight, bias_row, factor):
    height, columns, channels = proj.shape
    out_channels = weight.shape[1] // (factor * factor)
    flattened = jnp.dot(proj.reshape(-1, channels), weight, preferred_element_type=jnp.float32)
    flattened = flattened + jnp.tile(bias_row, factor * factor)[None, :]
    result = flattened.astype(jnp.bfloat16).reshape(height, columns, factor, factor, out_channels)
    return result.transpose(0, 2, 1, 3, 4).reshape(height * factor, columns * factor, out_channels)


def convolve(padded, weight, out_rows, out_cols):
    channels = padded.shape[2]
    total = jnp.zeros((out_rows, out_cols, weight.shape[3]), jnp.float32)
    for row_tap in range(3):
        for col_tap in range(3):
            window = padded[row_tap : row_tap + out_rows, col_tap : col_tap + out_cols]
            term = jnp.dot(
                window.reshape(-1, channels),
                weight[row_tap, col_tap],
                preferred_element_type=jnp.float32,
            )
            total = total + term.reshape(out_rows, out_cols, -1)
    return total.astype(jnp.bfloat16)


def project_one(tokens_block, weight, bias_row):
    projected = jnp.dot(tokens_block, weight, preferred_element_type=jnp.float32) + bias_row
    return projected.astype(jnp.bfloat16)


def body(
    hidden_states,
    cell_of,
    proj_four_weight,
    proj_four_bias,
    proj_two_weight,
    proj_two_bias,
    proj_same_weight,
    proj_same_bias,
    up4_weight,
    up4_bias,
    up2_weight,
    up2_bias,
    join_weight,
):
    tok_dev = hidden_states.shape[1]
    shards = lax.axis_size("rows")
    myself = lax.axis_index("rows")
    per_peer = tok_dev // shards
    my_cells = lax.dynamic_slice_in_dim(cell_of, myself * tok_dev, tok_dev)
    outgoing = jnp.argsort(my_cells // tok_dev, stable=True)
    table = cell_of.reshape(shards, tok_dev)
    foreign = (table // tok_dev != myself).astype(jnp.int32)
    picked = jnp.argsort(foreign, axis=1, stable=True)[:, :per_peer]
    arriving = jnp.take_along_axis(table, picked, axis=1).reshape(-1) - myself * tok_dev
    placing = jnp.argsort(arriving)
    pairs = (
        (proj_four_weight, proj_four_bias),
        (proj_two_weight, proj_two_bias),
        (proj_same_weight, proj_same_bias),
    )
    local_four = project_one(hidden_states[0][outgoing], pairs[0][0], pairs[0][1])
    local_two = project_one(hidden_states[1][outgoing], pairs[1][0], pairs[1][1])
    local_same = project_one(hidden_states[2][outgoing], pairs[2][0], pairs[2][1])
    arrived = side_by_side((local_four, local_two, local_same), "rows", 0, 0, 1)
    tiles = [piece[placing] for piece in arrived]
    row_count = tok_dev // GRID_W
    upsampled_four = expand(tiles[0].reshape(row_count, GRID_W, -1), up4_weight, up4_bias, 4)
    rimmed = with_halo(upsampled_four, (("rows", 0),), 1)
    padded = jnp.pad(rimmed, ((0, 0), (1, 1), (0, 0)))
    joined_four = convolve(padded, join_weight, 4 * row_count, 4 * GRID_W)
    upsampled_two = expand(tiles[1].reshape(row_count, GRID_W, -1), up2_weight, up2_bias, 2)
    same_scale = tiles[2].reshape(row_count, GRID_W, -1)
    return (joined_four, upsampled_two, same_scale)


def solution(mesh):
    return jax.shard_map(
        body,
        mesh=mesh,
        in_specs=(
            P(None, ("img", "rows"), None),
            P(),
            P(),
            P(),
            P(),
            P(),
            P(),
            P(),
            P(),
            P(),
            P(),
            P(),
            P(),
        ),
        out_specs=(
            P(("img", "rows"), None, None),
            P(("img", "rows"), None, None),
            P(("img", "rows"), None, None),
        ),
        check_vma=False,
    )
```

profile of v0, /device:TPU:37, one launch (start us, length us, event | category | flops | bytes accessed | tf_op | source)
XLA Modules:
  0.0 156.3 jit_solution(13384962224604230756)
XLA Ops:
  7.2 0.9 and_select_fusion
  8.1 2.5 %sort.51 = (s32[128]{0:T(128)}, s32[128]{0:T(128)S(1)}) sort(s32[128]{0:T(128)S(1)} %and_select_fusion, s32[128]{0:T(128)S(1)} %iota.15), dimensions={0}, to_apply=%region_0.1 | sort | flops 896 | bytes 2048 | tf_op jit(solution)/shard_map/jit(argsort)/sort | solution.py:88
  10.7 1.2 slice_bitcast_fusion.2
  11.8 0.9 gather_fusion.2
  12.7 0.9 gather_fusion.1
  13.6 1.6 %gather_fusion = bf16[128,1024]{1,0:T(8,128)(2,1)} fusion(bf16[128,1024]{1,0:T(8,128)(2,1)S(1)} %get-tuple-element.11, s32[1024]{0:T(1024)S(1)} %pad_clamp_fusion.1), kind=kCustom, calls=%fused_computation | custom fusion | bytes 524800 | tf_op jit(solution)/shard_map/gather | solution.py:99
  15.2 2.2 %fusion.8 = bf16[128,1024]{1,0:T(8,128)(2,1)S(1)} fusion(bf16[128,1024]{1,0:T(8,128)(2,1)S(1)} %gather_fusion.2, bf16[1024,1024]{1,0:T(8,128)(2,1)} %param.19, f32[1024]{0:T(1024)S(1)} %copy-done.9), kind=kOutput, calls=%fused_computation.21 | convolution fusion | flops 268697600 | bytes 2625536 | tf_op jit(solution)/shard_map/dot_general | solution.py:64
  17.4 0.3 fusion.17
  17.7 0.2 fusion.18
  18.0 0.9 all_to_all.8
  19.0 34.3 %all-to-all-start = ((bf16[64,2,1792]{2,1,0:T(2,128)(2,1)}), bf16[64,2,1792]{2,1,0:T(2,128)(2,1)S(1)}, u32[]{:S(2)}, u32[]{:S(2)}) async-start(bf16[64,2,1792]{2,1,0:T(2,128)(2,1)} %all_to_all.8), calls=%async_computation | async-start | bytes 917504 | tf_op jit(solution)/shard_map/all_to_all | solution.py:12
  53.4 0.6 fusion.55
  54.0 0.6 iota.16
  54.8 5.6 %sort.55.cloned.1.call-done = (s32[64,128]{1,0:T(8,128)}, s32[64,128]{1,0:T(8,128)}) async-done(((s32[64,128]{1,0:T(8,128)}, s32[64,128]{1,0:T(8,128)}), (s32[64,128]{1,0:T(8,128)}, s32[64,128]{1,0:T(8,128)})) %sort.55.cloned.1.call-update) | async-done | bytes 65552 | tf_op jit(solution)/shard_map/jit(argsort)/sort | solution.py:91
  60.4 0.8 clamp_shift-left_fusion
  61.2 0.1 copy.21
  61.3 0.1 reshape.141
  61.5 1.2 gather_fusion.6
  62.7 0.1 reshape.144
  62.9 0.1 sub.25
  63.1 2.5 %sort.53 = (s32[128]{0:T(128)}, s32[128]{0:T(128)S(1)}) sort(s32[128]{0:T(128)S(1)} %sub.25, s32[128]{0:T(128)S(1)} %iota.17), dimensions={0}, to_apply=%region_2.3 | sort | flops 896 | bytes 2048 | tf_op jit(solution)/shard_map/jit(argsort)/sort | solution.py:93
  65.6 46.0 %all-to-all-done = bf16[64,2,1792]{2,1,0:T(2,128)(2,1)S(1)} async-done(((bf16[64,2,1792]{2,1,0:T(2,128)(2,1)}), bf16[64,2,1792]{2,1,0:T(2,128)(2,1)S(1)}, u32[]{:S(2)}, u32[]{:S(2)}) %all-to-all-start) | async-done | bytes 458784 | tf_op jit(solution)/shard_map/all_to_all | solution.py:12
  111.6 0.2 all_to_all.10
  111.8 0.8 gather_fusion.3
  112.7 1.4 fusion
  114.1 2.6 %reshape.88 = bf16[2,64,4,4,256]{4,3,2,1,0:T(4,128)(2,1)} reshape(bf16[128,4096]{1,0:T(8,128)(2,1)} %fusion) | data formatting | bytes 2097152 | tf_op jit(solution)/shard_map/reshape | solution.py:44
  116.7 2.6 %copy.22 = bf16[2,4,64,4,256]{4,3,2,1,0:T(4,128)(2,1)} copy(bf16[2,4,64,4,256]{4,3,1,2,0:T(4,128)(2,1)} %bitcast.78) | data formatting | bytes 2097152 | tf_op jit(solution)/shard_map/transpose | solution.py:45
  119.3 1.3 reshape.89
  120.7 0.7 fusion.58
  121.4 3.8 %collective-permute-start = (bf16[1,256,256]{2,1,0:T(8,128)(2,1)}, bf16[1,256,256]{2,1,0:T(8,128)(2,1)S(1)}, u32[]{:S(2)}, u32[]{:S(2)}) collective-permute-start(bf16[1,256,256]{2,1,0:T(8,128)(2,1)} %get-tuple-element.9), channel_id=1, source_target_pairs={{0,1},{1,2},{2,3},{3,4},{4,5},{5,6},{6,7},{7,8},{8,9},{9,10},{10,1... | collective-permute-start | bytes 393224 | tf_op jit(solution)/shard_map/ppermute | solution.py:30
  125.2 2.1 %collective-permute-start.1 = (bf16[1,256,256]{2,1,0:T(8,128)(2,1)}, bf16[1,256,256]{2,1,0:T(8,128)(2,1)}, u32[]{:S(2)}, u32[]{:S(2)}) collective-permute-start(bf16[1,256,256]{2,1,0:T(8,128)(2,1)} %get-tuple-element.10), channel_id=1, source_target_pairs={{1,0},{2,1},{3,2},{4,3},{5,4},{6,5},{7,6},{8,7},{9,8},{10,9},{11,1... | collective-permute-start | bytes 393224 | tf_op jit(solution)/shard_map/ppermute | solution.py:32
  127.4 2.7 %fusion.37 = f32[8,256,256]{2,1,0:T(8,128)} fusion(bf16[8,256,256]{2,1,0:T(8,128)(2,1)S(1)} %reshape.89, bf16[3,3,256,256]{3,2,1,0:T(8,128)(2,1)} %param.25), kind=kOutput, calls=%fused_computation.54 | convolution fusion | flops 268435456 | bytes 3276800 | tf_op jit(solution)/shard_map/dot_general | solution.py:54
  130.1 0.8 gather_fusion.4
  130.9 2.8 %fusion.2 = bf16[128,2048]{1,0:T(8,128)(2,1)} fusion(bf16[128,512]{1,0:T(8,128)(2,1)S(1)} %gather_fusion.4, bf16[512,2048]{1,0:T(8,128)(2,1)} %param.23, f32[2048]{0:T(1024)S(1)} %bitcast.82), kind=kOutput, calls=%fused_computation.13 | convolution fusion | flops 268959744 | bytes 2760704 | tf_op jit(solution)/shard_map/dot_general | solution.py:42
  133.7 2.3 %reshape.90 = bf16[2,64,2,2,512]{4,3,2,1,0:T(2,128)(2,1)} reshape(bf16[128,2048]{1,0:T(8,128)(2,1)} %fusion.2) | data formatting | bytes 1048576 | tf_op jit(solution)/shard_map/reshape | solution.py:44
  136.0 2.2 %copy.23 = bf16[2,2,64,2,512]{4,3,2,1,0:T(2,128)(2,1)} copy(bf16[2,2,64,2,512]{4,3,1,2,0:T(2,128)(2,1)} %bitcast.79) | data formatting | bytes 1048576 | tf_op jit(solution)/shard_map/transpose | solution.py:45
  138.2 2.0 %reshape.91 = bf16[4,128,512]{2,1,0:T(8,128)(2,1)} reshape(bf16[2,2,64,2,512]{4,3,2,1,0:T(2,128)(2,1)} %copy.23) | data formatting | bytes 1048576 | tf_op jit(solution)/shard_map/reshape | solution.py:45
  140.2 1.6 gather_fusion.5
  141.8 1.3 fusion.7
  143.2 0.4 fusion.23
  143.6 0.5 fusion.25
  144.0 0.4 fusion.27
  144.5 0.5 fusion.29
  144.9 0.4 fusion.31
  145.4 0.4 fusion.9
  145.8 1.5 fusion.13
  147.3 0.2 copy-done.3
  147.4 2.0 %add_convert_fusion = bf16[8,256,256]{2,1,0:T(8,128)(2,1)} fusion(f32[8,256,256]{2,1,0:T(8,128)S(1)} %fusion.13, f32[8,256,256]{2,1,0:T(8,128)S(1)} %fusion.23, f32[8,256,256]{2,1,0:T(8,128)S(1)} %fusion.25, f32[8,256,256]{2,1,0:T(8,128)S(1)} %copy-done.3, f32[8,256,256]{2,1,0:T(8,128)S(1)} %fusion.27, f32[8,256,256]{2,1,0:T(8,128)S(1)} %fusion.29, ...), kind=kOutput, calls=%fused_computation.14 | convolution fusion | flops 273154048 | bytes 19005440 | tf_op jit(solution)/shard_map/dot_general | solution.py:54
  (50 shorter events, 0.4 us)
Async XLA Ops:
  7.2 105.5 %copy-start = (bf16[256,4096]{1,0:T(8,128)(2,1)S(1)}, bf16[256,4096]{1,0:T(8,128)(2,1)}, u32[]{:S(2)}) copy-start(bf16[256,4096]{1,0:T(8,128)(2,1)} %param.21) | copy-start | bytes 6291460
  12.7 2.4 %copy-start.9 = (f32[1024]{0:T(1024)S(1)}, f32[1024]{0:T(1024)}, u32[]{:S(2)}) copy-start(f32[1024]{0:T(1024)} %param.20) | copy-start | bytes 12292
  13.6 3.8 %copy-start.10 = (f32[512]{0:T(512)S(1)}, f32[512]{0:T(512)}, u32[]{:S(2)}) copy-start(f32[512]{0:T(512)} %param.18) | copy-start | bytes 6148
  15.1 2.2 %copy-start.5 = (bf16[1024,512]{1,0:T(8,128)(2,1)S(1)}, bf16[1024,512]{1,0:T(8,128)(2,1)}, u32[]{:S(2)}) copy-start(bf16[1024,512]{1,0:T(8,128)(2,1)} %param.17) | copy-start | bytes 3145732
  15.1 2.5 %copy-start.6 = (bf16[128,1024]{1,0:T(8,128)(2,1)S(1)}, bf16[128,1024]{1,0:T(8,128)(2,1)}, u32[]{:S(2)}) copy-start(bf16[128,1024]{1,0:T(8,128)(2,1)} %gather_fusion) | copy-start | bytes 786436
  15.1 2.5 %copy-start.7 = (bf16[1024,256]{1,0:T(8,128)(2,1)S(1)}, bf16[1024,256]{1,0:T(8,128)(2,1)}, u32[]{:S(2)}) copy-start(bf16[1024,256]{1,0:T(8,128)(2,1)} %param.15) | copy-start | bytes 1572868
  15.2 2.5 %copy-start.12 = (f32[256]{0:T(256)S(1)}, f32[256]{0:T(256)}, u32[]{:S(2)}) copy-start(f32[256]{0:T(256)} %param.16) | copy-start | bytes 3076
  17.7 35.7 %copy-start.1 = (s32[8192]{0:T(1024)S(1)}, s32[8192]{0:T(1024)}, u32[]{:S(2)}) copy-start(s32[8192]{0:T(1024)} %param.14) | copy-start | bytes 98308
  17.7 37.0 %copy-start.13 = (f32[256]{0:T(256)S(1)}, f32[256]{0:T(256)}, u32[]{:S(2)}) copy-start(f32[256]{0:T(256)} %param.22) | copy-start | bytes 3076
  17.7 37.0 %copy-start.11 = (f32[512]{0:T(512)S(1)}, f32[512]{0:T(512)}, u32[]{:S(2)}) copy-start(f32[512]{0:T(512)} %param.24) | copy-start | bytes 6148
  19.0 92.7 %all-to-all-start = ((bf16[64,2,1792]{2,1,0:T(2,128)(2,1)}), bf16[64,2,1792]{2,1,0:T(2,128)(2,1)S(1)}, u32[]{:S(2)}, u32[]{:S(2)}) async-start(bf16[64,2,1792]{2,1,0:T(2,128)(2,1)} %all_to_all.8), calls=%async_computation | async-start | bytes 917504 | tf_op jit(solution)/shard_map/all_to_all | solution.py:12
  53.3 7.1 %sort.55.cloned.1.call-start = ((), (), s32[]{:S(2)}) async-start(), calls=%async_computation.1 | async-start | bytes 196640 | tf_op jit(solution)/shard_map/jit(argsort)/sort | solution.py:91
  61.5 1.4 copy-start.8
  111.8 2.3 %copy-start.2 = (bf16[128,1792]{1,0:T(8,128)(2,1)}, bf16[128,1792]{1,0:T(8,128)(2,1)S(1)}, u32[]{:S(2)}) copy-start(bf16[128,1792]{1,0:T(8,128)(2,1)S(1)} %all_to_all.10) | copy-start | bytes 1376260
  120.7 9.4 %slice-start = ((bf16[128,1792]{1,0:T(8,128)(2,1)}), bf16[128,512]{1,0:T(8,128)(2,1)S(1)}, s32[]{:S(2)}) async-start(bf16[128,1792]{1,0:T(8,128)(2,1)} %copy-done.2), calls=%async_computation.3 | async-start | bytes 262144 | tf_op jit(solution)/shard_map/slice | solution.py:17
  121.4 20.4 %collective-permute-start = (bf16[1,256,256]{2,1,0:T(8,128)(2,1)}, bf16[1,256,256]{2,1,0:T(8,128)(2,1)S(1)}, u32[]{:S(2)}, u32[]{:S(2)}) collective-permute-start(bf16[1,256,256]{2,1,0:T(8,128)(2,1)} %get-tuple-element.9), channel_id=1, source_target_pairs={{0,1},{1,2},{2,3},{3,4},{4,5},{5,6},{6,7},{7,8},{8,9},{9,10},{10,1... | collective-permute-start | bytes 393224 | tf_op jit(solution)/shard_map/ppermute | solution.py:30
  125.2 16.6 %collective-permute-start.1 = (bf16[1,256,256]{2,1,0:T(8,128)(2,1)}, bf16[1,256,256]{2,1,0:T(8,128)(2,1)}, u32[]{:S(2)}, u32[]{:S(2)}) collective-permute-start(bf16[1,256,256]{2,1,0:T(8,128)(2,1)} %get-tuple-element.10), channel_id=1, source_target_pairs={{1,0},{2,1},{3,2},{4,3},{5,4},{6,5},{7,6},{8,7},{9,8},{10,9},{11,1... | collective-permute-start | bytes 393224 | tf_op jit(solution)/shard_map/ppermute | solution.py:32
  133.7 6.5 %slice-start.1 = ((bf16[128,1792]{1,0:T(8,128)(2,1)}), bf16[128,1024]{1,0:T(8,128)(2,1)S(1)}, s32[]{:S(2)}) async-start(bf16[128,1792]{1,0:T(8,128)(2,1)} %copy-done.2), calls=%async_computation.4 | async-start | bytes 524288 | tf_op jit(solution)/shard_map/slice | solution.py:17
  141.8 1.3 copy-start.4
  145.8 1.7 %copy-start.3 = (f32[8,256,256]{2,1,0:T(8,128)S(1)}, f32[8,256,256]{2,1,0:T(8,128)}, u32[]{:S(2)}) copy-start(f32[8,256,256]{2,1,0:T(8,128)} %fusion.37) | copy-start | bytes 6291460
Sparse Core Ops, SparseCore 0:
  57.0 3.1 sort.57.cloned.1.call-done
  (1 shorter events, 0.0 us)
where the time goes:
time: 157 us; the launch traced here: 156 us
  waiting for transfers between devices  46 us (29%)
  starting transfers between devices  40.3 us (26%)
  local copies, waits for them, and re-layouts  31 us (20%)
  matrix products  15.8 us (10%)
  between operations  14.4 us (9%)
  other arithmetic  8.81 us (6%)
    all_to_all x1, waiting for transfers between devices, side_by_side(): lax.all_to_all(both, axis, split_axis=split_dim, concat_axis=concat_dim,...  46 us
    all_to_all x1, starting transfers between devices, side_by_side(): lax.all_to_all(both, axis, split_axis=split_dim, concat_axis=concat_dim,...  34.3 us
    dot_general x9, matrix products, convolve(): jnp.dot(window.reshape(-1, channels), weight[row_tap, col_tap], preferred...  8.79 us
    sort x2, local copies, waits for them, and re-layouts, body(): picked = jnp.argsort(foreign, axis=1, stable=True)[:, :per_peer]  5.65 us
    reshape x2, local copies, waits for them, and re-layouts, expand(): flattened.astype(jnp.bfloat16)  4.89 us
    transpose x2, local copies, waits for them, and re-layouts, expand(): result.transpose(0, 2, 1, 3, 4)  4.77 us
    dot_general x2, matrix products, expand(): jnp.dot(proj.reshape(-1, channels), weight, preferred_element_type=jnp.fl...  4.25 us
    ppermute x1, starting transfers between devices, with_halo(): lax.ppermute(tail, axis, [(i, (i + 1) % count) for i in range(ends)])  3.83 us
  transfers between devices with their start and end apart: 3, of which 1 were waited for; matrix products, arithmetic and copies ran while one was open for 13% of the time, Pallas kernels for 0%

commit v1 on v0

v1 whole, which is shorter than its diff:
```python
import functools

import jax
import jax.numpy as jnp
from jax import lax
from jax.experimental import pallas as pl
from jax.experimental.pallas import tpu as pltpu
from jax.sharding import PartitionSpec as P

GRID_W = 64
F32 = jnp.float32
BF16 = jnp.bfloat16


def dot(a, b):
    return jnp.dot(a, b, preferred_element_type=F32)


def dot_first(a, b):
    return lax.dot_general(a, b, (((0,), (0,)), ((), ())), preferred_element_type=F32)


def iota(shape, dim):
    return lax.broadcasted_iota(jnp.int32, shape, dim)


def one_hot(mask):
    return jnp.where(mask, 1.0, 0.0).astype(BF16)


def kernel(
    shards,
    hidden_hbm,
    cells_hbm,
    w4_hbm,
    b4_hbm,
    w2_hbm,
    b2_hbm,
    w1_hbm,
    b1_hbm,
    u4_hbm,
    c4_hbm,
    u2_hbm,
    c2_hbm,
    join_hbm,
    joined_hbm,
    up2_hbm,
    same_hbm,
    hidden,
    cells,
    w4,
    b4,
    w2,
    b2,
    w1,
    b1,
    u4,
    c4,
    u2,
    c2,
    join,
    in4,
    in2,
    in1,
    send4,
    send2,
    send1,
    edge,
    rim,
    phases,
    mixed,
    joined,
    wide,
    same,
    load_sem,
    send_sem,
    recv_sem,
    edge_send,
    edge_recv,
    store_sem,
):
    me = lax.axis_index("rows")
    tile = hidden.shape[1]
    half = tile // 2

    def remote(src, dst, send, recv, peer):
        return pltpu.make_async_remote_copy(
            src_ref=src,
            dst_ref=dst,
            send_sem=send,
            recv_sem=recv,
            device_id={"rows": peer},
            device_id_type=pl.DeviceIdType.MESH,
        )

    loads = [
        pltpu.make_async_copy(src, dst, load_sem.at[k])
        for k, (src, dst) in enumerate(
            [
                (cells_hbm, cells),
                (hidden_hbm.at[0], hidden.at[0]),
                (w4_hbm, w4),
                (b4_hbm, b4),
                (hidden_hbm.at[1], hidden.at[1]),
                (w2_hbm, w2),
                (b2_hbm, b2),
                (hidden_hbm.at[2], hidden.at[2]),
                (w1_hbm, w1),
                (b1_hbm, b1),
                (u4_hbm, u4),
                (c4_hbm, c4),
                (join_hbm, join),
                (u2_hbm, u2),
                (c2_hbm, c2),
            ]
        )
    ]
    for load in loads:
        load.start()

    barrier = pltpu.get_barrier_semaphore()

    @pl.loop(1, shards)
    def _(k):
        pl.semaphore_signal(
            barrier,
            inc=1,
            device_id={"rows": lax.rem(me + k, shards)},
            device_id_type=pl.DeviceIdType.MESH,
        )

    loads[0].wait()
    mine = cells[pl.ds(me, 1), :]
    row = iota((tile, tile), 0)
    owner = lax.div(mine, tile) == lax.div(row, 2)
    low = jnp.min(jnp.where(owner, mine, shards * tile), axis=1, keepdims=True)
    outgoing = one_hot(owner & ((mine == low) == (lax.rem(row, 2) == 0)))

    table = cells[...]
    here = lax.div(table, tile) == me
    local = lax.rem(table, tile)
    first = jnp.min(jnp.where(here, local, tile), axis=1, keepdims=True)
    last = jnp.max(jnp.where(here, local, -1), axis=1, keepdims=True)
    twice = one_hot(lax.div(iota((tile, shards), 0), 2) == iota((tile, shards), 1))
    wide_first = dot(twice, jnp.broadcast_to(first, (shards, tile)).astype(F32).astype(BF16))
    wide_last = dot(twice, jnp.broadcast_to(last, (shards, tile)).astype(F32).astype(BF16))
    target = jnp.where(lax.rem(row, 2) == 0, wide_first, wide_last)
    placing = one_hot(target == iota((tile, tile), 1).astype(F32))

    def project(layer, weight, bias):
        value = dot(hidden[layer], weight[...]) + bias[...]
        return dot(outgoing, value.astype(BF16)).astype(BF16)

    sends = (send4, send2, send1)
    arrivals = (in4, in2, in1)

    def put(piece, value):
        sends[piece][...] = value.reshape(shards, 2, value.shape[1])

    def launch(piece):
        @pl.loop(1, shards)
        def _(k):
            peer = lax.rem(me + k, shards)
            remote(
                sends[piece].at[peer],
                arrivals[piece].at[me],
                send_sem.at[piece],
                recv_sem.at[piece],
                peer,
            ).start()

        pltpu.make_async_copy(
            sends[piece].at[me], arrivals[piece].at[me], recv_sem.at[piece]
        ).start()

    for k in (1, 2, 3):
        loads[k].wait()
    put(0, project(0, w4, b4))
    for k in (4, 5, 6):
        loads[k].wait()
    put(1, project(1, w2, b2))
    pl.semaphore_wait(barrier, shards - 1)
    launch(0)
    launch(1)
    for k in (7, 8, 9):
        loads[k].wait()
    put(2, project(2, w1, b1))
    launch(2)

    def collect(piece):
        buffer = arrivals[piece]
        pltpu.make_async_copy(buffer, buffer, recv_sem.at[piece]).wait()
        value = buffer[...].reshape(tile, buffer.shape[2])
        return dot_first(placing, value).astype(BF16)

    tile4 = collect(0)
    edge[...] = tile4
    upper, lower = lax.max(me - 1, 0), lax.min(me + 1, shards - 1)
    to_upper = remote(
        edge.at[pl.ds(0, half)], rim.at[1], edge_send.at[0], edge_recv.at[1], upper
    )
    to_lower = remote(
        edge.at[pl.ds(half, half)], rim.at[0], edge_send.at[1], edge_recv.at[0], lower
    )

    @pl.when(me > 0)
    def _():
        to_upper.start()

    @pl.when(me < shards - 1)
    def _():
        to_lower.start()

    for k in (10, 11, 12):
        loads[k].wait()
    feat = c4.shape[1]
    column = lax.rem(iota((tile, feat), 0), half)

    def spread(value, phase, place):
        place(phase + 1, value)
        if phase == 3:
            rolled = pltpu.roll(value, 1, 0)
            place(0, jnp.where(column[: value.shape[0]] == 0, 0.0, rolled))
        if phase == 0:
            rolled = pltpu.roll(value, value.shape[0] - 1, 0)
            place(5, jnp.where(column[: value.shape[0]] == half - 1, 0.0, rolled))

    for a in range(4):
        for b in range(4):
            at = (a * 4 + b) * feat
            value = dot(tile4, u4[:, at : at + feat]) + c4[...]

            def place(slot, rows, a=a):
                rows = rows.astype(BF16)
                phases[slot, pl.ds((1 + a) * half, half), :] = rows[:half]
                phases[slot, pl.ds((5 + a) * half, half), :] = rows[half:]

            spread(value, b, place)

    @pl.when(me > 0)
    def _():
        to_upper.wait_send()
        to_lower.wait_recv()

    @pl.when(me < shards - 1)
    def _():
        to_lower.wait_send()
        to_upper.wait_recv()

    for side, a, keep, at_row in ((0, 3, me > 0, 0), (1, 0, me < shards - 1, 9)):

        @pl.when(keep)
        def _():
            for b in range(4):
                at = (a * 4 + b) * feat
                value = dot(rim[side], u4[:, at : at + feat]) + c4[...]

                def place(slot, rows):
                    phases[slot, pl.ds(at_row * half, half), :] = rows.astype(BF16)

                spread(value, b, place)

        @pl.when(jnp.logical_not(keep))
        def _():
            for slot in range(6):
                phases[slot, pl.ds(at_row * half, half), :] = jnp.zeros((half, feat), BF16)

    @pl.loop(0, 4)
    def _(phase):
        taps = []
        for a in range(3):
            for b in range(3):
                taps.append(phases[phase + b, pl.ds(a * half, 8 * half), :])
        value = dot(jnp.concatenate(taps, axis=1), join[...])
        mixed[phase] = value.astype(BF16).reshape(8, half, value.shape[1])

    order = iota((4 * half, 4 * half), 0)
    source = iota((4 * half, 4 * half), 1)
    weave4 = one_hot(source == lax.rem(order, 4) * half + lax.div(order, 4))

    @pl.loop(0, 8)
    def _(r):
        columns = mixed[:, r].reshape(4 * half, mixed.shape[3])
        joined[r] = dot(weave4, columns).astype(BF16)
        pltpu.make_async_copy(joined.at[r], joined_hbm.at[r], store_sem.at[0]).start()

    tile2 = collect(1)
    for k in (13, 14):
        loads[k].wait()
    weave2 = one_hot(
        iota((tile, tile), 1) == lax.rem(row, 2) * half + lax.div(row, 2)
    )
    c_two = c2.shape[1]
    for a in range(2):
        pair = [
            (dot(tile2, u2[:, at : at + c_two]) + c2[...]).astype(BF16)
            for at in ((a * 2) * c_two, (a * 2 + 1) * c_two)
        ]
        for i in range(2):
            both = jnp.concatenate([p[i * half : (i + 1) * half] for p in pair], axis=0)
            wide[2 * i + a] = dot(weave2, both).astype(BF16)
    pltpu.make_async_copy(wide, up2_hbm, store_sem.at[1]).start()

    tile1 = collect(2)
    same[...] = tile1.reshape(2, half, tile1.shape[1])
    pltpu.make_async_copy(same, same_hbm, store_sem.at[2]).start()

    for piece in range(3):
        most = sends[piece].at[pl.ds(0, shards - 1)]
        pltpu.make_async_copy(most, most, send_sem.at[piece]).wait()
    pltpu.make_async_copy(joined, joined_hbm, store_sem.at[0]).wait()
    pltpu.make_async_copy(wide, up2_hbm, store_sem.at[1]).wait()
    pltpu.make_async_copy(same, same_hbm, store_sem.at[2]).wait()


def body(
    hidden_states,
    cell_of,
    proj_four_weight,
    proj_four_bias,
    proj_two_weight,
    proj_two_bias,
    proj_same_weight,
    proj_same_bias,
    up4_weight,
    up4_bias,
    up2_weight,
    up2_bias,
    join_weight,
):
    shards = lax.axis_size("rows")
    tile = hidden_states.shape[1]
    half = tile // 2
    four, two, one = (
        proj_four_weight.shape[1],
        proj_two_weight.shape[1],
        proj_same_weight.shape[1],
    )
    feat = join_weight.shape[3]
    operands = (
        hidden_states,
        cell_of.reshape(shards, tile),
        proj_four_weight,
        proj_four_bias.reshape(1, -1),
        proj_two_weight,
        proj_two_bias.reshape(1, -1),
        proj_same_weight,
        proj_same_bias.reshape(1, -1),
        up4_weight,
        up4_bias.reshape(1, -1),
        up2_weight,
        up2_bias.reshape(1, -1),
        join_weight.reshape(-1, feat),
    )
    vmem = pltpu.VMEM
    return tuple(
        pl.pallas_call(
            functools.partial(kernel, shards),
            out_shape=(
                jax.ShapeDtypeStruct((8, 4 * half, feat), BF16),
                jax.ShapeDtypeStruct((4, 2 * half, two), BF16),
                jax.ShapeDtypeStruct((2, half, one), BF16),
            ),
            in_specs=[pl.BlockSpec(memory_space=pltpu.HBM)] * len(operands),
            out_specs=[pl.BlockSpec(memory_space=pltpu.HBM)] * 3,
            scratch_shapes=[vmem(o.shape, o.dtype) for o in operands]
            + [
                vmem((shards, 2, four), BF16),
                vmem((shards, 2, two), BF16),
                vmem((shards, 2, one), BF16),
                vmem((shards, 2, four), BF16),
                vmem((shards, 2, two), BF16),
                vmem((shards, 2, one), BF16),
                vmem((tile, four), BF16),
                vmem((2, half, four), BF16),
                vmem((6, 10 * half, four), BF16),
                vmem((4, 8, half, feat), BF16),
                vmem((8, 4 * half, feat), BF16),
                vmem((4, 2 * half, two), BF16),
                vmem((2, half, one), BF16),
                pltpu.SemaphoreType.DMA((15,)),
                pltpu.SemaphoreType.DMA((3,)),
                pltpu.SemaphoreType.DMA((3,)),
                pltpu.SemaphoreType.DMA((2,)),
                pltpu.SemaphoreType.DMA((2,)),
                pltpu.SemaphoreType.DMA((3,)),
            ],
            compiler_params=pltpu.CompilerParams(
                collective_id=0, has_side_effects=True, vmem_limit_bytes=66_000_000
            ),
            name="pyramid",
        )(*operands)
    )


def solution(mesh):
    rows = P(("img", "rows"), None, None)
    return jax.shard_map(
        body,
        mesh=mesh,
        in_specs=(P(None, ("img", "rows"), None),) + (P(),) * 12,
        out_specs=(rows,) * 3,
        check_vma=False,
    )
```

time: 157 us -> 86.6 us (0.55)
  Pallas kernels: 0 us -> 82 us
  waiting for transfers between devices: 46 us -> 0 us
  starting transfers between devices: 40.3 us -> 0 us
  local copies, waits for them, and re-layouts: 31 us -> 3.84 us
  matrix products: 15.8 us -> 0 us
  between operations: 14.4 us -> 0.66 us
  other arithmetic: 8.81 us -> 0 us
    pallas_call x0 -> x1, Pallas kernels: none -> 82 us  [body(): pl.pallas_call(functools.partial(kernel, shards), out_shape=(jax.ShapeDty...]
    all_to_all x1 -> x0, waiting for transfers between devices: 46 us -> none  [side_by_side(): lax.all_to_all(both, axis, split_axis=split_dim, concat_axis=concat_dim,...]
    all_to_all x1 -> x0, starting transfers between devices: 34.3 us -> none  [side_by_side(): lax.all_to_all(both, axis, split_axis=split_dim, concat_axis=concat_dim,...]
    dot_general x14 -> x0, matrix products: 15.8 us -> none  [the longest x9 8.79 us: convolve(): jnp.dot(window.reshape(-1, channels), weight[row_tap, col_tap], preferred...]
    reshape x4 -> x0, local copies, waits for them, and re-layouts: 8.26 us -> none  [the longest x2 4.89 us: expand(): flattened.astype(jnp.bfloat16)]
    gather x11 -> x0, local copies, waits for them, and re-layouts: 8.23 us -> none  [the longest x3 3.26 us: body(): tiles = [piece[placing] for piece in arrived]]
    ppermute x2 -> x0, starting transfers between devices: 5.96 us -> none  [the longest x1 3.83 us: with_halo(): lax.ppermute(tail, axis, [(i, (i + 1) % count) for i in range(ends)])]
    sort x2 -> x0, local copies, waits for them, and re-layouts: 5.65 us -> none  [body(): picked = jnp.argsort(foreign, axis=1, stable=True)[:, :per_peer]]
  transfers between devices with their start and end apart: 3 -> 0, of which waited for: 1 -> 0; matrix products, arithmetic and copies ran while one was open for 13% -> 0% of each run, Pallas kernels for 0% -> 0%
where the time goes in v1:
time: 86.6 us; the launch traced here: 86.5 us
  Pallas kernels  82 us (95%)
  local copies, waits for them, and re-layouts  3.84 us (4%)
    pallas_call x1, Pallas kernels, body(): pl.pallas_call(functools.partial(kernel, shards), out_shape=(jax.ShapeDty...  82 us
    unnamed x7, local copies, waits for them, and re-layouts  3.84 us

profile of v1, /device:TPU:37, one launch (start us, length us, event | category | flops | bytes accessed | tf_op | source)
XLA Modules:
  0.0 86.5 jit_solution(11309036424368905491)
XLA Ops:
  0.6 82.0 %pyramid.1 = (bf16[8,256,256]{2,1,0:T(8,128)(2,1)}, bf16[4,128,512]{2,1,0:T(8,128)(2,1)}, bf16[2,64,1024]{2,1,0:T(8,128)(2,1)}) custom-call(bf16[3,128,1024]{2,1,0:T(8,128)(2,1)} %hidden_hbm.1, s32[64,128]{1,0:T(8,128)} %bitcast.8, bf16[1024,256]{1,0:T(8,128)(2,1)} %w4_hbm.1, f32[1,256]{1,0:T(1,128)} %bitcast.12, bf16[1024,512]{1,0:T(8,128)(2,1)} %w2_hbm.1, ...), custom_call_target="tpu_custom_call" | custom-call | tf_op jit(solution)/shard_map/pyramid/pallas_call | solution.py:357
  82.7 0.0 copy-start
  82.7 0.0 copy-start.1
  82.7 2.3 %copy.19 = bf16[8,256,256]{2,1,0:T(8,128)(2,1)} copy(bf16[8,256,256]{2,1,0:T(8,128)(2,1)} %get-tuple-element.6) | data formatting | bytes 2097152
  85.0 0.0 copy-done
  85.0 0.8 copy.20
  85.8 0.0 copy-done.1
  85.8 0.7 copy.21
Async XLA Ops:
  82.7 2.4 %copy-start = (bf16[4,128,512]{2,1,0:T(8,128)(2,1)S(1)}, bf16[4,128,512]{2,1,0:T(8,128)(2,1)}, u32[]{:S(2)}) copy-start(bf16[4,128,512]{2,1,0:T(8,128)(2,1)} %get-tuple-element.7) | copy-start | bytes 1572868
  82.7 3.1 %copy-start.1 = (bf16[2,64,1024]{2,1,0:T(8,128)(2,1)S(1)}, bf16[2,64,1024]{2,1,0:T(8,128)(2,1)}, u32[]{:S(2)}) copy-start(bf16[2,64,1024]{2,1,0:T(8,128)(2,1)} %get-tuple-element.8) | copy-start | bytes 786436

commit v2 on v1

--- a/solution.py
+++ b/solution.py
@@ -8,6 +8,7 @@
 from jax.sharding import PartitionSpec as P
 
 GRID_W = 64
+NEAR = 4
 F32 = jnp.float32
 BF16 = jnp.bfloat16
 
@@ -78,6 +79,7 @@
     edge_send,
     edge_recv,
     store_sem,
+    known_sem,
 ):
     me = lax.axis_index("rows")
     tile = hidden.shape[1]
@@ -119,15 +121,36 @@
         load.start()
 
     barrier = pltpu.get_barrier_semaphore()
-
-    @pl.loop(1, shards)
-    def _(k):
+    chips = shards // 2
+    z = lax.div(me, 2)
+    core = lax.rem(me, 2)
+    rounds = chips // 2 // NEAR
+
+    def signal(sem, peer):
         pl.semaphore_signal(
-            barrier,
-            inc=1,
-            device_id={"rows": lax.rem(me + k, shards)},
-            device_id_type=pl.DeviceIdType.MESH,
+            sem, inc=1, device_id={"rows": peer}, device_id_type=pl.DeviceIdType.MESH
         )
+
+    def around(d):
+        return lax.rem(z + d + chips, chips)
+
+    signal(barrier, me + 1 - 2 * core)
+
+    @pl.loop(1, NEAR + 1)
+    def _(d):
+        for side in (d, -d):
+            for other in range(2):
+                signal(barrier, 2 * around(side) + other)
+
+    def known(k):
+        if k == 0:
+            pl.semaphore_wait(barrier, 4 * NEAR + 1)
+        else:
+            pl.semaphore_wait(known_sem.at[2 * k - 2], 1)
+            pl.semaphore_wait(known_sem.at[2 * k - 1], 1)
+        if k < rounds - 1:
+            signal(known_sem.at[2 * k], 2 * around(NEAR) + core)
+            signal(known_sem.at[2 * k + 1], 2 * around(-NEAR) + core)
 
     loads[0].wait()
     mine = cells[pl.ds(me, 1), :]
@@ -140,10 +163,10 @@
     here = lax.div(table, tile) == me
     local = lax.rem(table, tile)
     first = jnp.min(jnp.where(here, local, tile), axis=1, keepdims=True)
-    last = jnp.max(jnp.where(here, local, -1), axis=1, keepdims=True)
+    final = jnp.max(jnp.where(here, local, -1), axis=1, keepdims=True)
     twice = one_hot(lax.div(iota((tile, shards), 0), 2) == iota((tile, shards), 1))
     wide_first = dot(twice, jnp.broadcast_to(first, (shards, tile)).astype(F32).astype(BF16))
-    wide_last = dot(twice, jnp.broadcast_to(last, (shards, tile)).astype(F32).astype(BF16))
+    wide_last = dot(twice, jnp.broadcast_to(final, (shards, tile)).astype(F32).astype(BF16))
     target = jnp.where(lax.rem(row, 2) == 0, wide_first, wide_last)
     placing = one_hot(target == iota((tile, tile), 1).astype(F32))
 
@@ -157,21 +180,39 @@
     def put(piece, value):
         sends[piece][...] = value.reshape(shards, 2, value.shape[1])
 
-    def launch(piece):
-        @pl.loop(1, shards)
-        def _(k):
-            peer = lax.rem(me + k, shards)
-            remote(
-                sends[piece].at[peer],
-                arrivals[piece].at[me],
-                send_sem.at[piece],
-                recv_sem.at[piece],
-                peer,
-            ).start()
-
+    def fling(pieces, chip):
+        for other in range(2):
+            for piece in pieces:
+                remote(
+                    sends[piece].at[2 * chip + other],
+                    arrivals[piece].at[me],
+                    send_sem.at[piece],
+                    recv_sem.at[piece],
+                    2 * chip + other,
+                ).start()
+
+    def home(piece):
         pltpu.make_async_copy(
             sends[piece].at[me], arrivals[piece].at[me], recv_sem.at[piece]
         ).start()
+        peer = me + 1 - 2 * core
+        remote(
+            sends[piece].at[peer],
+            arrivals[piece].at[me],
+            send_sem.at[piece],
+            recv_sem.at[piece],
+            peer,
+        ).start()
+
+    def spanning(pieces, low, high, down=True):
+        @pl.loop(0, high - low + 1)
+        def _(k):
+            d = high - k if down else low + k
+            fling(pieces, around(d))
+
+            @pl.when(d < chips // 2)
+            def _():
+                fling(pieces, around(-d))
 
     for k in (1, 2, 3):
         loads[k].wait()
@@ -179,13 +220,20 @@
     for k in (4, 5, 6):
         loads[k].wait()
     put(1, project(1, w2, b2))
-    pl.semaphore_wait(barrier, shards - 1)
-    launch(0)
-    launch(1)
     for k in (7, 8, 9):
         loads[k].wait()
     put(2, project(2, w1, b1))
-    launch(2)
+    known(0)
+    spanning((0, 1, 2), 1, 4)
+    known(1)
+    spanning((0, 1), 5, 8)
+    known(2)
+    spanning((0, 1), 9, 12)
+    known(3)
+    spanning((0,), 13, 16)
+    spanning((1, 2), 13, 16)
+    for piece in range(3):
+        home(piece)
 
     def collect(piece):
         buffer = arrivals[piece]
@@ -211,6 +259,7 @@
     def _():
         to_lower.start()
 
+    spanning((2,), 5, 12)
     for k in (10, 11, 12):
         loads[k].wait()
     feat = c4.shape[1]
@@ -384,6 +433,7 @@
                 pltpu.SemaphoreType.DMA((2,)),
                 pltpu.SemaphoreType.DMA((2,)),
                 pltpu.SemaphoreType.DMA((3,)),
+                pltpu.SemaphoreType.REGULAR((8,)),
             ],
             compiler_params=pltpu.CompilerParams(
                 collective_id=0, has_side_effects=True, vmem_limit_bytes=66_000_000

time: 86.6 us -> 75.5 us (0.87)
  Pallas kernels: 82 us -> 70.9 us
    pallas_call x1, Pallas kernels: 82 us -> 70.9 us  [body(): pl.pallas_call(functools.partial(kernel, shards), out_shape=(jax.ShapeDty...]
where the time goes in v2:
time: 75.5 us; the launch traced here: 75.4 us
  Pallas kernels  70.9 us (94%)
  local copies, waits for them, and re-layouts  3.84 us (5%)
    pallas_call x1, Pallas kernels, body(): pl.pallas_call(functools.partial(kernel, shards), out_shape=(jax.ShapeDty...  70.9 us
    unnamed x7, local copies, waits for them, and re-layouts  3.84 us

profile of v2, /device:TPU:37, one launch (start us, length us, event | category | flops | bytes accessed | tf_op | source)
XLA Modules:
  0.0 75.4 jit_solution(7998551456044617146)
XLA Ops:
  0.6 70.9 %pyramid.1 = (bf16[8,256,256]{2,1,0:T(8,128)(2,1)}, bf16[4,128,512]{2,1,0:T(8,128)(2,1)}, bf16[2,64,1024]{2,1,0:T(8,128)(2,1)}) custom-call(bf16[3,128,1024]{2,1,0:T(8,128)(2,1)} %hidden_hbm.1, s32[64,128]{1,0:T(8,128)} %bitcast.8, bf16[1024,256]{1,0:T(8,128)(2,1)} %w4_hbm.1, f32[1,256]{1,0:T(1,128)} %bitcast.12, bf16[1024,512]{1,0:T(8,128)(2,1)} %w2_hbm.1, ...), custom_call_target="tpu_custom_call" | custom-call | tf_op jit(solution)/shard_map/pyramid/pallas_call | solution.py:406
  71.5 0.0 copy-start
  71.5 0.0 copy-start.1
  71.6 2.3 %copy.19 = bf16[8,256,256]{2,1,0:T(8,128)(2,1)} copy(bf16[8,256,256]{2,1,0:T(8,128)(2,1)} %get-tuple-element.6) | data formatting | bytes 2097152
  73.9 0.0 copy-done
  73.9 0.8 %copy.20 = bf16[4,128,512]{2,1,0:T(8,128)(2,1)} copy(bf16[4,128,512]{2,1,0:T(8,128)(2,1)S(1)} %copy-done) | data formatting | bytes 1048576
  74.7 0.0 copy-done.1
  74.7 0.7 copy.21
Async XLA Ops:
  71.5 2.4 %copy-start = (bf16[4,128,512]{2,1,0:T(8,128)(2,1)S(1)}, bf16[4,128,512]{2,1,0:T(8,128)(2,1)}, u32[]{:S(2)}) copy-start(bf16[4,128,512]{2,1,0:T(8,128)(2,1)} %get-tuple-element.7) | copy-start | bytes 1572868
  71.5 3.1 %copy-start.1 = (bf16[2,64,1024]{2,1,0:T(8,128)(2,1)S(1)}, bf16[2,64,1024]{2,1,0:T(8,128)(2,1)}, u32[]{:S(2)}) copy-start(bf16[2,64,1024]{2,1,0:T(8,128)(2,1)} %get-tuple-element.8) | copy-start | bytes 786436

commit v3 on v2

--- a/solution.py
+++ b/solution.py
@@ -44,9 +44,9 @@
     u2_hbm,
     c2_hbm,
     join_hbm,
-    joined_hbm,
-    up2_hbm,
-    same_hbm,
+    joined,
+    wide,
+    same,
     hidden,
     cells,
     w4,
@@ -70,15 +70,11 @@
     rim,
     phases,
     mixed,
-    joined,
-    wide,
-    same,
     load_sem,
     send_sem,
     recv_sem,
     edge_send,
     edge_recv,
-    store_sem,
     known_sem,
 ):
     me = lax.axis_index("rows")
@@ -331,7 +327,6 @@
     def _(r):
         columns = mixed[:, r].reshape(4 * half, mixed.shape[3])
         joined[r] = dot(weave4, columns).astype(BF16)
-        pltpu.make_async_copy(joined.at[r], joined_hbm.at[r], store_sem.at[0]).start()
 
     tile2 = collect(1)
     for k in (13, 14):
@@ -348,18 +343,22 @@
         for i in range(2):
             both = jnp.concatenate([p[i * half : (i + 1) * half] for p in pair], axis=0)
             wide[2 * i + a] = dot(weave2, both).astype(BF16)
-    pltpu.make_async_copy(wide, up2_hbm, store_sem.at[1]).start()
 
     tile1 = collect(2)
     same[...] = tile1.reshape(2, half, tile1.shape[1])
-    pltpu.make_async_copy(same, same_hbm, store_sem.at[2]).start()
 
     for piece in range(3):
         most = sends[piece].at[pl.ds(0, shards - 1)]
         pltpu.make_async_copy(most, most, send_sem.at[piece]).wait()
-    pltpu.make_async_copy(joined, joined_hbm, store_sem.at[0]).wait()
-    pltpu.make_async_copy(wide, up2_hbm, store_sem.at[1]).wait()
-    pltpu.make_async_copy(same, same_hbm, store_sem.at[2]).wait()
+
+
+def keep(joined, wide, same, joined_hbm, up2_hbm, same_hbm, sems):
+    pairs = ((joined, joined_hbm), (wide, up2_hbm), (same, same_hbm))
+    copies = [pltpu.make_async_copy(a, b, sems.at[k]) for k, (a, b) in enumerate(pairs)]
+    for copy in copies:
+        copy.start()
+    for copy in copies:
+        copy.wait()
 
 
 def body(
@@ -402,44 +401,49 @@
         join_weight.reshape(-1, feat),
     )
     vmem = pltpu.VMEM
+    operands = [pltpu.with_memory_space_constraint(o, pltpu.HBM) for o in operands]
+    results = pl.pallas_call(
+        functools.partial(kernel, shards),
+        out_shape=(
+            vmem((8, 4 * half, feat), BF16),
+            vmem((4, 2 * half, two), BF16),
+            vmem((2, half, one), BF16),
+        ),
+        in_specs=[pl.BlockSpec(memory_space=pltpu.HBM)] * len(operands),
+        out_specs=[pl.BlockSpec(memory_space=pltpu.VMEM)] * 3,
+        scratch_shapes=[vmem(o.shape, o.dtype) for o in operands]
+        + [
+            vmem((shards, 2, four), BF16),
+            vmem((shards, 2, two), BF16),
+            vmem((shards, 2, one), BF16),
+            vmem((shards, 2, four), BF16),
+            vmem((shards, 2, two), BF16),
+            vmem((shards, 2, one), BF16),
+            vmem((tile, four), BF16),
+            vmem((2, half, four), BF16),
+            vmem((6, 10 * half, four), BF16),
+            vmem((4, 8, half, feat), BF16),
+            pltpu.SemaphoreType.DMA((15,)),
+            pltpu.SemaphoreType.DMA((3,)),
+            pltpu.SemaphoreType.DMA((3,)),
+            pltpu.SemaphoreType.DMA((2,)),
+            pltpu.SemaphoreType.DMA((2,)),
+            pltpu.SemaphoreType.REGULAR((8,)),
+        ],
+        compiler_params=pltpu.CompilerParams(
+            collective_id=0, has_side_effects=True, vmem_limit_bytes=63_000_000
+        ),
+        name="pyramid",
+    )(*operands)
     return tuple(
         pl.pallas_call(
-            functools.partial(kernel, shards),
-            out_shape=(
-                jax.ShapeDtypeStruct((8, 4 * half, feat), BF16),
-                jax.ShapeDtypeStruct((4, 2 * half, two), BF16),
-                jax.ShapeDtypeStruct((2, half, one), BF16),
-            ),
-            in_specs=[pl.BlockSpec(memory_space=pltpu.HBM)] * len(operands),
+            keep,
+            out_shape=[jax.ShapeDtypeStruct(r.shape, r.dtype) for r in results],
+            in_specs=[pl.BlockSpec(memory_space=pltpu.VMEM)] * 3,
             out_specs=[pl.BlockSpec(memory_space=pltpu.HBM)] * 3,
-            scratch_shapes=[vmem(o.shape, o.dtype) for o in operands]
-            + [
-                vmem((shards, 2, four), BF16),
-                vmem((shards, 2, two), BF16),
-                vmem((shards, 2, one), BF16),
-                vmem((shards, 2, four), BF16),
-                vmem((shards, 2, two), BF16),
-                vmem((shards, 2, one), BF16),
-                vmem((tile, four), BF16),
-                vmem((2, half, four), BF16),
-                vmem((6, 10 * half, four), BF16),
-                vmem((4, 8, half, feat), BF16),
-                vmem((8, 4 * half, feat), BF16),
-                vmem((4, 2 * half, two), BF16),
-                vmem((2, half, one), BF16),
-                pltpu.SemaphoreType.DMA((15,)),
-                pltpu.SemaphoreType.DMA((3,)),
-                pltpu.SemaphoreType.DMA((3,)),
-                pltpu.SemaphoreType.DMA((2,)),
-                pltpu.SemaphoreType.DMA((2,)),
-                pltpu.SemaphoreType.DMA((3,)),
-                pltpu.SemaphoreType.REGULAR((8,)),
-            ],
-            compiler_params=pltpu.CompilerParams(
-                collective_id=0, has_side_effects=True, vmem_limit_bytes=66_000_000
-            ),
-            name="pyramid",
-        )(*operands)
+            scratch_shapes=[pltpu.SemaphoreType.DMA((3,))],
+            name="keep",
+        )(*[pltpu.with_memory_space_constraint(r, pltpu.VMEM) for r in results])
     )
 
 

time: 75.5 us -> 72.2 us (0.956)
  local copies, waits for them, and re-layouts: 3.84 us -> 0 us
    unnamed x7 -> x0, local copies, waits for them, and re-layouts: 3.84 us -> none
    pallas_call x1 -> x2, Pallas kernels: 70.9 us -> 71.4 us  [the longest x1 70.2 us: body(): pl.pallas_call(functools.partial(kernel, shards), out_shape=(vmem((8, 4 *...]
where the time goes in v3:
time: 72.2 us; the launch traced here: 72.1 us
  Pallas kernels  71.4 us (99%)
    pallas_call x1, Pallas kernels, body(): pl.pallas_call(functools.partial(kernel, shards), out_shape=(vmem((8, 4 *...  70.2 us

profile of v3, /device:TPU:37, one launch (start us, length us, event | category | flops | bytes accessed | tf_op | source)
XLA Modules:
  0.0 72.1 jit_solution(8254125559455396397)
XLA Ops:
  0.6 70.2 %pyramid.1 = (bf16[8,256,256]{2,1,0:T(8,128)(2,1)S(1)}, bf16[4,128,512]{2,1,0:T(8,128)(2,1)S(1)}, bf16[2,64,1024]{2,1,0:T(8,128)(2,1)S(1)}) custom-call(bf16[3,128,1024]{2,1,0:T(8,128)(2,1)} %hidden_hbm.1, s32[64,128]{1,0:T(8,128)} %bitcast.8, bf16[1024,256]{1,0:T(8,128)(2,1)} %w4_hbm.1, f32[1,256]{1,0:T(1,128)} %bitcast.12, bf16[1024,512]{1,0:T(8,128)(2,1)} %w2_hbm.1, ...), custom_call_target="tpu_custom_call" | custom-call | tf_op jit(solution)/shard_map/pyramid/pallas_call | solution.py:405
  70.8 1.2 %keep.1 = (bf16[8,256,256]{2,1,0:T(8,128)(2,1)}, bf16[4,128,512]{2,1,0:T(8,128)(2,1)}, bf16[2,64,1024]{2,1,0:T(8,128)(2,1)}) custom-call(bf16[8,256,256]{2,1,0:T(8,128)(2,1)S(1)} %get-tuple-element.6.joined, bf16[4,128,512]{2,1,0:T(8,128)(2,1)S(1)} %get-tuple-element.7.wide, bf16[2,64,1024]{2,1,0:T(8,128)(2,1)S(1)} %get-tuple-element.8.same), custom_call_target="tpu_custom_call" | custom-call | tf_op jit(solution)/shard_map/keep/pallas_call | solution.py:439

commit v4 on v3

--- a/solution.py
+++ b/solution.py
@@ -113,7 +113,7 @@
             ]
         )
     ]
-    for load in loads:
+    for load in loads[:10]:
         load.start()
 
     barrier = pltpu.get_barrier_semaphore()
@@ -227,7 +227,10 @@
     spanning((0, 1), 9, 12)
     known(3)
     spanning((0,), 13, 16)
-    spanning((1, 2), 13, 16)
+    spanning((1,), 13, 16)
+    spanning((2,), 13, 16)
+    for load in loads[10:]:
+        load.start()
     for piece in range(3):
         home(piece)
 
@@ -237,6 +240,13 @@
         value = buffer[...].reshape(tile, buffer.shape[2])
         return dot_first(placing, value).astype(BF16)
 
+    def sent(piece):
+        most = sends[piece].at[pl.ds(0, shards - 1)]
+        pltpu.make_async_copy(most, most, send_sem.at[piece]).wait()
+
+    sent(0)
+    sent(1)
+    spanning((2,), 11, 12)
     tile4 = collect(0)
     edge[...] = tile4
     upper, lower = lax.max(me - 1, 0), lax.min(me + 1, shards - 1)
@@ -255,7 +265,7 @@
     def _():
         to_lower.start()
 
-    spanning((2,), 5, 12)
+    spanning((2,), 5, 10)
     for k in (10, 11, 12):
         loads[k].wait()
     feat = c4.shape[1]
@@ -347,14 +357,13 @@
     tile1 = collect(2)
     same[...] = tile1.reshape(2, half, tile1.shape[1])
 
-    for piece in range(3):
-        most = sends[piece].at[pl.ds(0, shards - 1)]
-        pltpu.make_async_copy(most, most, send_sem.at[piece]).wait()
+    sent(2)
 
 
 def keep(joined, wide, same, joined_hbm, up2_hbm, same_hbm, sems):
     pairs = ((joined, joined_hbm), (wide, up2_hbm), (same, same_hbm))
-    copies = [pltpu.make_async_copy(a, b, sems.at[k]) for k, (a, b) in enumerate(pairs)]
+    rows = [(a.at[r], b.at[r]) for a, b in pairs for r in range(a.shape[0])]
+    copies = [pltpu.make_async_copy(a, b, sems.at[k]) for k, (a, b) in enumerate(rows)]
     for copy in copies:
         copy.start()
     for copy in copies:
@@ -441,7 +450,7 @@
             out_shape=[jax.ShapeDtypeStruct(r.shape, r.dtype) for r in results],
             in_specs=[pl.BlockSpec(memory_space=pltpu.VMEM)] * 3,
             out_specs=[pl.BlockSpec(memory_space=pltpu.HBM)] * 3,
-            scratch_shapes=[pltpu.SemaphoreType.DMA((3,))],
+            scratch_shapes=[pltpu.SemaphoreType.DMA((sum(r.shape[0] for r in results),))],
             name="keep",
         )(*[pltpu.with_memory_space_constraint(r, pltpu.VMEM) for r in results])
     )

time: 72.2 us -> 71.9 us (level)
  no operation moved by 1% of the time
where the time goes in v4:
time: 71.9 us; the launch traced here: 71.8 us
  Pallas kernels  71.2 us (99%)
    pallas_call x1, Pallas kernels, body(): pl.pallas_call(functools.partial(kernel, shards), out_shape=(vmem((8, 4 *...  69.8 us

profile of v4, /device:TPU:37, one launch (start us, length us, event | category | flops | bytes accessed | tf_op | source)
XLA Modules:
  0.0 71.8 jit_solution(13692109000790630885)
XLA Ops:
  0.6 69.8 %pyramid.1 = (bf16[8,256,256]{2,1,0:T(8,128)(2,1)S(1)}, bf16[4,128,512]{2,1,0:T(8,128)(2,1)S(1)}, bf16[2,64,1024]{2,1,0:T(8,128)(2,1)S(1)}) custom-call(bf16[3,128,1024]{2,1,0:T(8,128)(2,1)} %hidden_hbm.1, s32[64,128]{1,0:T(8,128)} %bitcast.8, bf16[1024,256]{1,0:T(8,128)(2,1)} %w4_hbm.1, f32[1,256]{1,0:T(1,128)} %bitcast.12, bf16[1024,512]{1,0:T(8,128)(2,1)} %w2_hbm.1, ...), custom_call_target="tpu_custom_call" | custom-call | tf_op jit(solution)/shard_map/pyramid/pallas_call | solution.py:414
  70.5 1.3 %keep.1 = (bf16[8,256,256]{2,1,0:T(8,128)(2,1)}, bf16[4,128,512]{2,1,0:T(8,128)(2,1)}, bf16[2,64,1024]{2,1,0:T(8,128)(2,1)}) custom-call(bf16[8,256,256]{2,1,0:T(8,128)(2,1)S(1)} %get-tuple-element.6.joined, bf16[4,128,512]{2,1,0:T(8,128)(2,1)S(1)} %get-tuple-element.7.wide, bf16[2,64,1024]{2,1,0:T(8,128)(2,1)S(1)} %get-tuple-element.8.same), custom_call_target="tpu_custom_call" | custom-call | tf_op jit(solution)/shard_map/keep/pallas_call | solution.py:448
